TPU v7x, 32 devices: a whole 2x2x4 slice. The times are simulated.
32 devices in a mesh: paths: 4 (over x, core), cpty: 8 (over z, y).
Axes of the slice: x: 2, y: 2, z: 4, core: 2. Of those that a mesh axis runs over, the one named last changes fastest.
Arguments:
- factors: bfloat16 [64, 6144], P(None, 'paths'), may hold values from -6 to 6
- loadings: bfloat16 [64, 16384], P(None, 'cpty'), may hold values from -2 to 2
- notional: bfloat16 [16384], P('cpty'), may hold values from 0.25 to 0.796875
- strike: bfloat16 [16384], P('cpty'), may hold values from 2 to 8
- curvature: bfloat16 [16384], P('cpty'), may hold values from 1 to 3
- trade_cpty: int32 [16384], P('cpty'), may hold values from 0 to 1023, as said below
Outputs:
- exposure: bfloat16 [6144, 1024], P('paths', 'cpty')
- moment: float32 [1024, 1024], P('paths', 'cpty')
Inputs may be any that keep to these rules, and one draw needn't show every extreme that they name: `trade_cpty`: of the trades in the book of one index of cpty, at most 512 belong to the counterparties numbered k * 128 to (k + 1) * 128 - 1 for any k; in every draw some such k receives exactly 512 from every book.
All inputs are finite; a program needn't handle non-finite values.
Results may differ from a plain program's by a relative error of at most 0.0064.
Values may be sent and summed in bfloat16 or wider, within the bound.
No kernel may reach another device: no remote copies, remote signals or barrier semaphores. Data moves between devices by JAX's collectives and lax.ppermute only.
A program may use at most 128 MiB of HBM per device.

v0:
```python
import jax
import jax.numpy as jnp
from jax import lax
from jax.sharding import PartitionSpec as P

CP_DEV = 128


def price_trades(drivers, loading_cols, trade_terms):
    linear = jnp.dot(drivers, loading_cols, preferred_element_type=jnp.float32)
    terms_wide = trade_terms.astype(jnp.float32)
    value = terms_wide[0] * (linear + terms_wide[2] * jnp.tanh(linear - terms_wide[1]))
    return value.astype(jnp.bfloat16)


def on_device(factors, loadings, notional, strike, curvature, trade_cpty):
    groups = lax.axis_size("cpty")
    own_index = lax.axis_index("cpty")
    trades = loadings.shape[1]
    slot_size = 2 * trades // groups
    owners = trade_cpty // CP_DEV
    marked = (owners[:, None] == jnp.arange(groups, dtype=jnp.int32)[None, :]).astype(jnp.int32)
    ranking = jnp.sum((jnp.cumsum(marked, axis=0) - marked) * marked, axis=1)
    target = owners * slot_size + ranking
    chosen = (
        jnp.zeros((groups * slot_size,), jnp.int32)
        .at[target]
        .set(jnp.arange(trades, dtype=jnp.int32))
    )
    filled = jnp.zeros((groups * slot_size,), jnp.bool_).at[target].set(True)
    labels = jnp.where(filled, trade_cpty[chosen], -1)[None, :]
    drivers = jnp.transpose(factors)
    trade_terms = jnp.stack([notional, strike, curvature])
    described = jnp.concatenate([loadings, trade_terms], axis=0)
    packed = jnp.where(
        filled[None, :], jnp.take(described, chosen, axis=1), jnp.zeros((), jnp.bfloat16)
    )
    received, arrived_ids = (
        lax.all_to_all(packed, "cpty", split_axis=1, concat_axis=1, tiled=True),
        lax.all_to_all(labels, "cpty", split_axis=1, concat_axis=1, tiled=True),
    )
    factor_count = loadings.shape[0]
    arrived = price_trades(drivers, received[:factor_count], received[factor_count:])
    local_ids = arrived_ids[0] - own_index * CP_DEV
    onehot = (local_ids[:, None] == jnp.arange(CP_DEV, dtype=jnp.int32)[None, :]).astype(
        jnp.bfloat16
    )
    netted = jnp.dot(arrived, onehot, preferred_element_type=jnp.float32)
    exposure = jnp.maximum(netted, 0.0).astype(jnp.bfloat16)
    everyone = lax.all_gather(exposure, "cpty", axis=1, tiled=True)
    path_total = exposure.shape[0] * lax.axis_size("paths")
    moment = (
        lax.psum_scatter(
            jnp.einsum("pa,pb->ab", everyone, exposure, preferred_element_type=jnp.float32),
            "paths",
            scatter_dimension=0,
            tiled=True,
        )
        / path_total
    )
    return (exposure, moment)


def solution(mesh):
    in_specs = (P(None, "paths"), P(None, "cpty"), P("cpty"), P("cpty"), P("cpty"), P("cpty"))
    out_specs = (P("paths", "cpty"), P("paths", "cpty"))
    return jax.shard_map(
        on_device, mesh=mesh, in_specs=in_specs, out_specs=out_specs, check_vma=False
    )
```

profile of v0, /device:TPU:2, one launch (start us, length us, event | category | flops | bytes accessed | tf_op | source)
XLA Modules:
  0.0 202.3 jit_solution(14715116246756037690)
XLA Ops:
  7.2 0.0 copy-start
  7.2 0.0 copy-start.1
  7.2 0.8 add_select_fusion
  8.0 2.3 %reduce-window.6 = s32[8,16,128]{2,1,0:T(8,128)S(1)} reduce-window(s32[8,16,128]{2,1,0:T(8,128)S(1)} %fusion.14, s32[]{:T(128)} %constant.24.clone.1), window={size=1x1x128 pad=0_0x0_0x127_0}, to_apply=%region_0.1 | reduce-window | flops 2080768 | bytes 131076 | tf_op jit(solution)/shard_map/reduce-window
  10.3 0.3 slice_reduce_fusion
  10.5 0.2 reduce-window.9
  10.7 0.1 add_bitcast_fusion
  10.9 0.7 compare_select_fusion.1
  11.6 8.1 %scatter_custom_fusion.1 = s32[4096]{0:T(1024)S(1)} fusion(s32[2048]{0:T(1024)S(1)} %compare_select_fusion.1, s32[2048]{0:T(1024)S(1)} %iota.15, s32[]{:T(128)} %constant.24.clone.1), kind=kCustom, calls=%fused_computation.43 | custom fusion | bytes 16388 | tf_op jit(solution)/shard_map/scatter | solution.py:28
  19.7 0.0 copy-done.1
  19.7 0.0 copy-start.2
  19.7 0.0 copy-start.3
  19.7 0.0 copy-start.4
  19.7 0.0 copy-start.5
  19.7 23.0 %gather_fusion.1 = s32[4096]{0:T(1024)S(1)} fusion(s32[2048]{0:T(1024)S(1)} %copy-done.1, s32[4096]{0:T(1024)S(1)} %fusion.15), kind=kCustom, calls=%fused_computation.1 | custom fusion | bytes 49152 | tf_op jit(solution)/shard_map/gather | solution.py:31
  42.8 9.1 %scatter_custom_fusion = pred[4096]{0:T(1024)(128)(4,1)S(1)} fusion(s32[2048]{0:T(1024)S(1)} %compare_select_fusion.1, pred[2048]{0:T(1024)(128)(4,1)S(1)} %broadcast.49, pred[]{:T(512)} %constant.22.clone.1), kind=kCustom, calls=%fused_computation.47 | custom fusion | bytes 4097 | tf_op jit(solution)/shard_map/scatter | solution.py:30
  51.9 0.6 broadcast_select_fusion
  52.5 5.8 %all-to-all-start.1 = ((s32[1,8,512]{2,0,1:T(1,128)}), s32[1,8,512]{2,0,1:T(1,128)S(1)}, u32[]{:S(2)}, u32[]{:S(2)}) async-start(s32[1,8,512]{2,0,1:T(1,128)} %bitcast.8), calls=%async_computation.1 | async-start | bytes 32768 | tf_op jit(solution)/shard_map/all_to_all | solution.py:40
  58.4 0.0 copy-done.2
  58.4 0.3 copy.19
  58.7 0.0 copy-done.3
  58.7 0.3 stack.12
  59.1 0.0 copy-done.4
  59.1 0.3 stack.13
  59.4 0.0 copy-done.5
  59.4 0.3 stack.14
  59.8 0.7 pad_maximum_fusion
  60.4 12.1 %gather_fusion = bf16[4096,67]{1,0:T(8,128)(2,1)S(1)} fusion(bf16[67,2048]{0,1:T(8,128)(2,1)S(1)} %pad_maximum_fusion, s32[4096]{0:T(1024)S(1)} %fusion.15), kind=kCustom, calls=%fused_computation | custom fusion | bytes 1114112 | tf_op jit(solution)/shard_map/jit(_take)/gather | solution.py:36
  72.6 0.6 copy.23
  73.2 0.9 select_select_fusion
  74.1 0.0 all-to-all-done.1
  74.1 6.0 %all-to-all-start = ((bf16[67,8,512]{2,0,1:T(8,128)(2,1)}), bf16[67,8,512]{2,0,1:T(8,128)(2,1)S(1)}, u32[]{:S(2)}, u32[]{:S(2)}) async-start(bf16[67,8,512]{2,0,1:T(8,128)(2,1)} %select_select_fusion), calls=%async_computation | async-start | bytes 1179648 | tf_op jit(solution)/shard_map/all_to_all | solution.py:39
  80.1 0.0 all-gather.2.cloned.1.call-start
  80.1 0.9 iota_compare_fusion.7
  81.0 14.4 %all-to-all-done = bf16[67,8,512]{2,0,1:T(8,128)(2,1)S(1)} async-done(((bf16[67,8,512]{2,0,1:T(8,128)(2,1)}), bf16[67,8,512]{2,0,1:T(8,128)(2,1)S(1)}, u32[]{:S(2)}, u32[]{:S(2)}) %all-to-all-start) | async-done | bytes 548896 | tf_op jit(solution)/shard_map/all_to_all | solution.py:39
  95.6 0.0 copy-done
  95.6 13.8 %fusion.9 = bf16[1536,128]{1,0:T(8,128)(2,1)} fusion(bf16[64,4096]{1,0:T(8,128)(2,1)S(1)} %bitcast.70, bf16[64,1536]{1,0:T(8,128)(2,1)S(1)} %copy-done, f32[4096]{0:T(1024)S(1)} %bitcast.75, f32[4096]{0:T(1024)S(1)} %bitcast.76, f32[4096]{0:T(1024)S(1)} %bitcast.74, pred[4096,128]{1,0:T(32,128)(4,1)S(1)} %iota_compare_fusion.7), kind=kOutput, calls=%fused_computation.15 | convolution fusion | flops 2447769600 | bytes 1687552 | tf_op jit(solution)/shard_map/dot_general | solution.py:48
  109.4 0.0 all-gather.2.cloned.1.call-update
  109.4 0.0 reduce-scatter.2.cloned.1.call-start
  109.4 61.8 %all-gather.2.cloned.1.call-done = bf16[1536,1024]{1,0:T(8,128)(2,1)} async-done(((bf16[1536,128]{1,0:T(8,128)(2,1)}), bf16[1536,1024]{1,0:T(8,128)(2,1)}) %all-gather.2.cloned.1.call-update) | async-done | bytes 3145744 | tf_op jit(solution)/shard_map/all_gather | solution.py:50
  171.3 3.7 %fusion.24 = f32[1024,128]{1,0:T(8,128)} fusion(bf16[1536,1024]{1,0:T(8,128)(2,1)} %all-gather.2.cloned.1.call-done, bf16[1536,128]{1,0:T(8,128)(2,1)} %fusion.9), kind=kOutput, calls=%fused_computation.51 | convolution fusion | flops 402653184 | bytes 4063232 | tf_op jit(solution)/shard_map/pa,pb->ab/dot_general | solution.py:54
  175.0 0.0 reduce-scatter.2.cloned.1.call-update
  175.0 18.8 %reduce-scatter.2.cloned.1.call-done = f32[256,128]{1,0:T(8,128)} async-done(((f32[1024,128]{1,0:T(8,128)}), f32[256,128]{1,0:T(8,128)}) %reduce-scatter.2.cloned.1.call-update) | async-done | bytes 131088 | tf_op jit(solution)/shard_map/reduce_scatter | solution.py:53
  193.8 1.6 broadcast_multiply_fusion
  (13 shorter events, 0.2 us)
Async XLA Ops:
  7.2 88.4 %copy-start = (bf16[64,1536]{1,0:T(8,128)(2,1)S(1)}, bf16[64,1536]{1,0:T(8,128)(2,1)}, u32[]{:S(2)}) copy-start(bf16[64,1536]{1,0:T(8,128)(2,1)} %param.6) | copy-start | bytes 589828
  7.2 12.5 %copy-start.1 = (s32[2048]{0:T(1024)S(1)}, s32[2048]{0:T(1024)}, u32[]{:S(2)}) copy-start(s32[2048]{0:T(1024)} %param.11) | copy-start | bytes 24580
  19.7 38.7 %copy-start.2 = (bf16[64,2048]{1,0:T(8,128)(2,1)S(1)}, bf16[64,2048]{1,0:T(8,128)(2,1)}, u32[]{:S(2)}) copy-start(bf16[64,2048]{1,0:T(8,128)(2,1)} %param.7) | copy-start | bytes 786436
  19.7 39.0 %copy-start.3 = (bf16[2048]{0:T(1024)(128)(2,1)S(1)}, bf16[2048]{0:T(1024)(128)(2,1)}, u32[]{:S(2)}) copy-start(bf16[2048]{0:T(1024)(128)(2,1)} %param.8) | copy-start | bytes 12292
  19.7 39.4 %copy-start.4 = (bf16[2048]{0:T(1024)(128)(2,1)S(1)}, bf16[2048]{0:T(1024)(128)(2,1)}, u32[]{:S(2)}) copy-start(bf16[2048]{0:T(1024)(128)(2,1)} %param.9) | copy-start | bytes 12292
  19.7 39.7 %copy-start.5 = (bf16[2048]{0:T(1024)(128)(2,1)S(1)}, bf16[2048]{0:T(1024)(128)(2,1)}, u32[]{:S(2)}) copy-start(bf16[2048]{0:T(1024)(128)(2,1)} %param.10) | copy-start | bytes 12292
  52.5 21.6 %all-to-all-start.1 = ((s32[1,8,512]{2,0,1:T(1,128)}), s32[1,8,512]{2,0,1:T(1,128)S(1)}, u32[]{:S(2)}, u32[]{:S(2)}) async-start(s32[1,8,512]{2,0,1:T(1,128)} %bitcast.8), calls=%async_computation.1 | async-start | bytes 32768 | tf_op jit(solution)/shard_map/all_to_all | solution.py:40
  74.1 21.4 %all-to-all-start = ((bf16[67,8,512]{2,0,1:T(8,128)(2,1)}), bf16[67,8,512]{2,0,1:T(8,128)(2,1)S(1)}, u32[]{:S(2)}, u32[]{:S(2)}) async-start(bf16[67,8,512]{2,0,1:T(8,128)(2,1)} %select_select_fusion), calls=%async_computation | async-start | bytes 1179648 | tf_op jit(solution)/shard_map/all_to_all | solution.py:39
  80.1 91.2 %all-gather.2.cloned.1.call-start = ((), (), s32[]{:S(2)}) async-start(), calls=%async_computation.3 | async-start | bytes 3538944 | tf_op jit(solution)/shard_map/all_gather | solution.py:50
  109.4 84.5 %reduce-scatter.2.cloned.1.call-start = ((), (), s32[]{:S(2)}) async-start(), calls=%async_computation.4 | async-start | bytes 655360 | tf_op jit(solution)/shard_map/reduce_scatter | solution.py:53
Sparse Core Ops, SparseCore 0:
  109.5 61.7 all-gather.1
  175.2 18.6 reduce-scatter.1
where the time goes:
time: 205 us; the launch traced here: 202 us
  waiting for transfers between devices  95.1 us (46%)
  local copies, waits for them, and re-layouts  54.7 us (27%)
  matrix products  17.5 us (9%)
  between operations  14.3 us (7%)
  starting transfers between devices  11.9 us (6%)
  other arithmetic  8.76 us (4%)
    all_gather x1, waiting for transfers between devices, on_device(): everyone = lax.all_gather(exposure, 'cpty', axis=1, tiled=True)  61.8 us
    gather x1, local copies, waits for them, and re-layouts, on_device(): labels = jnp.where(filled, trade_cpty[chosen], -1)[None, :]  23 us
    reduce_scatter x1, waiting for transfers between devices, on_device(): lax.psum_scatter(jnp.einsum('pa,pb->ab', everyone, exposure, preferred_el...  18.8 us
    all_to_all x1, waiting for transfers between devices, on_device(): lax.all_to_all(packed, 'cpty', split_axis=1, concat_axis=1, tiled=True)  14.4 us
    dot_general x1, matrix products, on_device(): netted = jnp.dot(arrived, onehot, preferred_element_type=jnp.float32)  13.8 us
    gather x2, local copies, waits for them, and re-layouts, on_device(): jnp.take(described, chosen, axis=1)  12.7 us
    scatter x1, local copies, waits for them, and re-layouts, on_device(): filled = jnp.zeros((groups * slot_size,), jnp.bool_).at[target].set(True)  9.13 us
    scatter x1, local copies, waits for them, and re-layouts, on_device(): chosen = jnp.zeros((groups * slot_size,), jnp.int32).at[target].set(jnp.a...  8.06 us
  transfers between devices with their start and end apart: 4, of which 3 were waited for; matrix products, arithmetic and copies ran while one was open for 8% of the time, Pallas kernels for 0%

commit v1 on v0

v1 whole, which is shorter than its diff:
```python
import functools

import jax
import jax.numpy as jnp
from jax import lax
from jax.experimental import pallas as pl
from jax.experimental.pallas import tpu as pltpu
from jax.sharding import PartitionSpec as P

CP_DEV = 128
LANES = 128
SUBLANES = 8

VMEM = pl.BlockSpec(memory_space=pltpu.VMEM)
SMEM = pl.BlockSpec(memory_space=pltpu.SMEM)


def dot_nt(left, right):
    return lax.dot_general(left, right, (((1,), (1,)), ((), ())), preferred_element_type=jnp.float32)


def dot_tn(left, right):
    return lax.dot_general(left, right, (((0,), (0,)), ((), ())), preferred_element_type=jnp.float32)


def pack_kernel(core_ref, ids_ref, loadings_ref, terms_ref, out_ref, described_ref):
    groups, rows, half = out_ref.shape
    factor_count, trades = loadings_ref.shape
    ids = ids_ref[...]
    owners = ids // CP_DEV
    marked = lax.broadcasted_iota(jnp.int32, (groups, trades), 0) == owners
    ones = jnp.where(marked, 1.0, 0.0).astype(jnp.bfloat16)
    blocks = trades // LANES
    stacked = jnp.concatenate([ones[:, b * LANES:(b + 1) * LANES] for b in range(blocks)], axis=0)
    upper = lax.broadcasted_iota(jnp.int32, (LANES, LANES), 0) <= lax.broadcasted_iota(jnp.int32, (LANES, LANES), 1)
    counts = jnp.dot(stacked, jnp.where(upper, 1.0, 0.0).astype(jnp.bfloat16), preferred_element_type=jnp.float32)
    before = jnp.zeros((groups, 1), jnp.float32)
    ranks = []
    for b in range(blocks):
        counted = counts[b * groups:(b + 1) * groups] + before
        chosen = jnp.where(marked[:, b * LANES:(b + 1) * LANES], counted, 0.0)
        ranks.append(jnp.sum(chosen, axis=0, keepdims=True))
        before = counted[:, LANES - 1:]
    ranking = jnp.concatenate(ranks, axis=1).astype(jnp.int32) - 1 - core_ref[0] * half
    target = jnp.where((ranking >= 0) & (ranking < half), owners * half + ranking, -1)
    described_ref[0:factor_count, :] = loadings_ref[...]
    terms = terms_ref[...].astype(jnp.float32)
    local_ids = (ids - owners * CP_DEV).astype(jnp.float32)
    tail = jnp.concatenate([terms, local_ids, jnp.zeros((SUBLANES - 4, trades), jnp.float32)], axis=0)
    described_ref[factor_count:rows, :] = tail.astype(jnp.bfloat16)
    described = described_ref[...]
    for g in range(groups):
        slots = lax.broadcasted_iota(jnp.int32, (half, trades), 0) + g * half
        select = jnp.where(slots == target, 1.0, 0.0).astype(jnp.bfloat16)
        out_ref[g] = dot_nt(described, select).astype(jnp.bfloat16)


def price_kernel(drivers_ref, mine_ref, other_ref, out_ref):
    path_tile = drivers_ref.shape[0]
    factor_count = drivers_ref.shape[1]
    groups, _, half = mine_ref.shape
    drivers = drivers_ref[...]
    total = jnp.zeros((path_tile, CP_DEV), jnp.float32)
    for ref in (mine_ref, other_ref):
        for g in range(groups):
            slab = ref[g]
            terms = slab[factor_count:factor_count + SUBLANES].astype(jnp.float32)
            linear = jnp.dot(drivers, slab[:factor_count], preferred_element_type=jnp.float32)
            value = terms[0:1] * (linear + terms[2:3] * jnp.tanh(linear - terms[1:2]))
            ids = terms[3:4].astype(jnp.int32)
            onehot = jnp.where(lax.broadcasted_iota(jnp.int32, (CP_DEV, half), 0) == ids, 1.0, 0.0)
            total = total + dot_nt(value.astype(jnp.bfloat16), onehot.astype(jnp.bfloat16))
    out_ref[...] = jnp.maximum(total, 0.0).astype(jnp.bfloat16)


def moment_kernel(z_ref, own_ref, peers_ref, whole_ref, half_ref, out_ref, columns_ref):
    lines, block, _ = out_ref.shape
    paths = own_ref.shape[0]
    z = z_ref[0]
    columns_ref[:, 0:block] = own_ref[...]
    for e in range(peers_ref.shape[0]):
        columns_ref[:, (e + 1) * block:(e + 2) * block] = peers_ref[e]
    out_ref[...] = jnp.zeros(out_ref.shape, out_ref.dtype)
    columns = columns_ref[...]
    out_ref[z] = dot_tn(own_ref[...], columns).astype(out_ref.dtype)
    for d in range(1, lines // 2):
        out_ref[(z - d) % lines] = dot_tn(whole_ref[d - 1], columns).astype(out_ref.dtype)
    far = lines // 2
    start = jnp.where(z >= far, 0, paths // 2)
    facing = columns_ref[pl.ds(pl.multiple_of(start, SUBLANES), paths // 2), :]
    out_ref[(z + far) % lines] = dot_tn(half_ref[...], facing).astype(out_ref.dtype)


def final_kernel(y_ref, own_ref, swapped_ref, crossed_ref, out_ref, *, scale):
    depth, block, _ = out_ref.shape
    y = y_ref[0]
    for e in range(depth):
        kept = own_ref[:, 0:block] if e == 0 else swapped_ref[e - 1].astype(jnp.float32)
        k = (-e) % depth
        turned = crossed_ref[:, k * block:(k + 1) * block].astype(jnp.float32).T
        out_ref[(y + e) % depth] = (kept + turned) * scale


def on_device(factors, loadings, notional, strike, curvature, trade_cpty, *, path_tile_count):
    lines = lax.axis_size("paths")
    groups = lax.axis_size("cpty")
    depth = groups // lines
    path_index = lax.axis_index("paths")
    own_index = lax.axis_index("cpty")
    z, y = own_index // depth, own_index % depth
    factor_count, trades = loadings.shape
    paths = factors.shape[1]
    half = trades // groups
    rows = factor_count + SUBLANES
    big = pltpu.CompilerParams(vmem_limit_bytes=56 * 1024 * 1024)

    packed = pl.pallas_call(
        pack_kernel,
        out_shape=jax.ShapeDtypeStruct((groups, rows, half), jnp.bfloat16),
        in_specs=[SMEM, VMEM, VMEM, VMEM],
        out_specs=VMEM,
        scratch_shapes=[pltpu.VMEM((rows, trades), jnp.bfloat16)],
        compiler_params=big,
        name="pack",
    )(
        (path_index % 2).astype(jnp.int32)[None],
        trade_cpty[None, :],
        loadings,
        jnp.stack([notional, strike, curvature]),
    )
    mine = lax.all_to_all(packed, "cpty", split_axis=0, concat_axis=0, tiled=True)
    other = lax.ppermute(mine, "paths", [(i, i ^ 1) for i in range(lines)])

    drivers = jnp.transpose(factors)
    path_tile = paths // path_tile_count
    whole_block = pl.BlockSpec((groups, rows, half), lambda i: (0, 0, 0))
    exposure = pl.pallas_call(
        price_kernel,
        grid=(path_tile_count,),
        out_shape=jax.ShapeDtypeStruct((paths, CP_DEV), jnp.bfloat16),
        in_specs=[pl.BlockSpec((path_tile, factor_count), lambda i: (i, 0)), whole_block, whole_block],
        out_specs=pl.BlockSpec((path_tile, CP_DEV), lambda i: (i, 0)),
        compiler_params=big,
        name="price",
    )(drivers, mine, other)

    everyone = range(groups)
    peers = [
        lax.ppermute(exposure, "cpty", [(c, c - c % depth + (c + e) % depth) for c in everyone])
        for e in range(1, depth)
    ]
    wholes = [
        lax.ppermute(exposure, "cpty", [(c, (c + d * depth) % groups) for c in everyone])
        for d in range(1, lines // 2)
    ]
    far = lines // 2
    sent = lax.dynamic_slice_in_dim(exposure, jnp.where(z < far, 0, paths // 2), paths // 2, 0)
    facing = lax.ppermute(sent, "cpty", [(c, (c + far * depth) % groups) for c in everyone])
    partial = pl.pallas_call(
        moment_kernel,
        out_shape=jax.ShapeDtypeStruct((lines, CP_DEV, depth * CP_DEV), jnp.bfloat16),
        in_specs=[SMEM, VMEM, VMEM, VMEM, VMEM],
        out_specs=VMEM,
        scratch_shapes=[pltpu.VMEM((paths, depth * CP_DEV), jnp.bfloat16)],
        compiler_params=big,
        name="moment",
    )(z.astype(jnp.int32)[None], exposure, jnp.stack(peers), jnp.stack(wholes), facing)
    spread = lax.all_to_all(partial, "paths", split_axis=0, concat_axis=0, tiled=True)
    summed = jnp.sum(spread.astype(jnp.float32), axis=0)
    leaving = summed.astype(jnp.bfloat16)

    def flat(p, zz, yy):
        return p * groups + zz * depth + yy

    crossed = lax.ppermute(
        leaving,
        ("paths", "cpty"),
        [
            (flat(a, b, yy), flat(b, a, yy))
            for a in range(lines)
            for b in range(lines)
            for yy in range(depth)
            if a != b
        ],
    )
    swapped = [
        lax.ppermute(
            leaving[:, e * CP_DEV:(e + 1) * CP_DEV],
            "cpty",
            [(c, c - c % depth + (c - e) % depth) for c in everyone],
        )
        for e in range(1, depth)
    ]
    moment = pl.pallas_call(
        functools.partial(final_kernel, scale=1.0 / (paths * lines)),
        out_shape=jax.ShapeDtypeStruct((depth, CP_DEV, CP_DEV), jnp.float32),
        in_specs=[SMEM, VMEM, VMEM, VMEM],
        out_specs=VMEM,
        compiler_params=big,
        name="final",
    )(y.astype(jnp.int32)[None], summed, jnp.stack(swapped), crossed)
    return exposure, moment.reshape(depth * CP_DEV, CP_DEV)


def solution(mesh):
    in_specs = (P(None, "paths"), P(None, "cpty"), P("cpty"), P("cpty"), P("cpty"), P("cpty"))
    out_specs = (P("paths", "cpty"), P("paths", "cpty"))
    return jax.shard_map(
        functools.partial(on_device, path_tile_count=3),
        mesh=mesh,
        in_specs=in_specs,
        out_specs=out_specs,
        check_vma=False,
    )
```

time: 205 us -> 81.2 us (0.40); the launches traced: 202 us -> 80.7 us
  waiting for transfers between devices: 95.1 us -> 23.8 us
  local copies, waits for them, and re-layouts: 54.7 us -> 6.25 us
  blocking collectives: 0 us -> 24.6 us
  Pallas kernels: 0 us -> 18.6 us
  matrix products: 17.5 us -> 0 us
  between operations: 14.3 us -> 0.73 us
  other arithmetic: 8.76 us -> 0.68 us
  starting transfers between devices: 11.9 us -> 6.07 us
    all_gather x1 -> x0, waiting for transfers between devices: 61.8 us -> none  [on_device(): everyone = lax.all_gather(exposure, 'cpty', axis=1, tiled=True)]
    gather x3 -> x0, local copies, waits for them, and re-layouts: 35.8 us -> none  [the longest x1 23 us: on_device(): labels = jnp.where(filled, trade_cpty[chosen], -1)[None, :]]
    all_to_all x0 -> x2, blocking collectives: none -> 24.6 us  [the longest x1 16.3 us: on_device(): lax.all_to_all(packed, 'cpty', split_axis=0, concat_axis=0, tiled=True)]
    ppermute x0 -> x6, waiting for transfers between devices: none -> 23.8 us  [the longest x1 17.8 us: on_device(): lax.ppermute(sent, 'cpty', [(c, (c + far * depth) % groups) for c in ever...]
    reduce_scatter x1 -> x0, waiting for transfers between devices: 18.8 us -> none  [on_device(): lax.psum_scatter(jnp.einsum('pa,pb->ab', everyone, exposure, preferred_el...]
    pallas_call x0 -> x4, Pallas kernels: none -> 18.6 us  [the longest x1 9.2 us: on_device(): pl.pallas_call(price_kernel, grid=(path_tile_count,), out_shape=jax.Shape...]
    dot_general x2 -> x0, matrix products: 17.5 us -> none  [the longest x1 13.8 us: on_device(): netted = jnp.dot(arrived, onehot, preferred_element_type=jnp.float32)]
    scatter x2 -> x0, local copies, waits for them, and re-layouts: 17.2 us -> none  [the longest x1 9.13 us: on_device(): filled = jnp.zeros((groups * slot_size,), jnp.bool_).at[target].set(True)]
  transfers between devices with their start and end apart: 4 -> 6, of which waited for: 3 -> 4; matrix products, arithmetic and copies ran while one was open for 8% -> 2% of each run, Pallas kernels for 0% -> 0%
where the time goes in v1:
time: 81.2 us; the launch traced here: 80.7 us
  blocking collectives  24.6 us (30%)
  waiting for transfers between devices  23.8 us (29%)
  Pallas kernels  18.6 us (23%)
  local copies, waits for them, and re-layouts  6.25 us (8%)
  starting transfers between devices  6.07 us (7%)
    ppermute x1, waiting for transfers between devices, on_device(): lax.ppermute(sent, 'cpty', [(c, (c + far * depth) % groups) for c in ever...  17.8 us
    all_to_all x1, blocking collectives, on_device(): lax.all_to_all(packed, 'cpty', split_axis=0, concat_axis=0, tiled=True)  16.3 us
    pallas_call x1, Pallas kernels, on_device(): pl.pallas_call(price_kernel, grid=(path_tile_count,), out_shape=jax.Shape...  9.2 us
    all_to_all x1, blocking collectives, on_device(): lax.all_to_all(partial, 'paths', split_axis=0, concat_axis=0, tiled=True)  8.27 us
    unnamed x25, local copies, waits for them, and re-layouts  5.26 us
    pallas_call x1, Pallas kernels, on_device(): pl.pallas_call(pack_kernel, out_shape=jax.ShapeDtypeStruct((groups, rows,...  5.2 us
    ppermute x1, waiting for transfers between devices, on_device(): lax.ppermute(leaving[:, e * CP_DEV:(e + 1) * CP_DEV], 'cpty', [(c, c - c...  3.22 us
    ppermute x1, starting transfers between devices, on_device(): lax.ppermute(leaving, ('paths', 'cpty'), [(flat(a, b, yy), flat(b, a, yy)...  2.53 us
  transfers between devices with their start and end apart: 6, of which 4 were waited for; matrix products, arithmetic and copies ran while one was open for 2% of the time, Pallas kernels for 0%

profile of v1, /device:TPU:2, one launch (start us, length us, event | category | flops | bytes accessed | tf_op | source)
XLA Modules:
  0.0 80.7 jit_solution(5675348679439795568)
XLA Ops:
  0.6 0.0 copy-start.9
  0.6 0.7 copy-done.9
  1.3 0.0 copy-start.10
  1.3 0.7 copy-done.10
  2.0 0.0 copy-start.11
  2.0 0.7 copy-done.11
  2.7 0.6 pad_maximum_fusion.terms_ref
  3.3 5.2 %pack.1 = bf16[8,72,256]{2,1,0:T(8,128)(2,1)} custom-call(s32[1]{0:T(128)} %bitcast.1.core_ref, s32[1,2048]{1,0:T(1,128)} %bitcast.14, bf16[64,2048]{1,0:T(8,128)(2,1)} %loadings_ref.1, bf16[3,2048]{1,0:T(4,128)(2,1)} %pad_maximum_fusion.terms_ref), custom_call_target="tpu_custom_call" | custom-call | tf_op jit(solution)/shard_map/pack/pallas_call | solution.py:117
  8.6 0.0 copy-start.6
  8.6 16.3 %all_to_all.10.mine_ref = bf16[8,72,256]{2,1,0:T(8,128)(2,1)S(1)} all-to-all(bf16[8,72,256]{2,1,0:T(8,128)(2,1)} %pack.1), channel_id=1, replica_groups=mesh['paths'=4,'cpty'=8] {'cpty'}, dimensions={0} | all-to-all | bytes 589824 | tf_op jit(solution)/shard_map/all_to_all | solution.py:131
  24.9 0.0 copy-start.1
  24.9 0.0 collective-permute-start
  24.9 0.0 copy-done.6
  24.9 0.9 %copy.8 = bf16[64,1536]{0,1:T(8,128)(2,1)} copy(bf16[64,1536]{1,0:T(8,128)(2,1)S(1)} %copy-done.6) | data formatting | bytes 393216 | tf_op args[0]
  25.8 0.0 copy-done.1
  25.8 0.6 collective-permute-done.other_ref
  26.4 0.0 copy-start.4
  26.4 0.7 copy-done.4
  27.1 9.2 %price.1.own_ref = bf16[1536,128]{1,0:T(8,128)(2,1)} custom-call(bf16[1536,64]{1,0:T(8,128)(2,1)} %bitcast.9, bf16[8,72,256]{2,1,0:T(8,128)(2,1)} %copy-done.1, bf16[8,72,256]{2,1,0:T(8,128)(2,1)} %copy-done.4), custom_call_target="tpu_custom_call" | custom-call | tf_op jit(solution)/shard_map/price/pallas_call | solution.py:137
  36.4 0.7 collective-permute-start.2
  37.0 0.5 collective-permute-start.1
  37.5 1.0 %constant_dynamic-slice_fusion = bf16[768,128]{1,0:T(8,128)(2,1)S(1)} fusion(bf16[1536,128]{1,0:T(8,128)(2,1)} %price.1.own_ref, s32[]{:T(128)S(6)} %select_n.23), kind=kLoop, calls=%fused_computation.2 | loop fusion | bytes 393220 | tf_op jit(solution)/shard_map/dynamic_slice | solution.py:157
  38.5 1.6 %collective-permute-start.3 = (bf16[768,128]{1,0:T(8,128)(2,1)S(1)}, bf16[768,128]{1,0:T(8,128)(2,1)S(1)}, u32[]{:S(2)}, u32[]{:S(2)}) collective-permute-start(bf16[768,128]{1,0:T(8,128)(2,1)S(1)} %constant_dynamic-slice_fusion), channel_id=1, source_target_pairs={{0,4},{1,5},{2,6},{3,7},{4,0},{5,1},{6,2},{7,3},{8,12},{9,13},{10,... | collective-permute-start | bytes 589832 | tf_op jit(solution)/shard_map/ppermute | solution.py:158
  40.1 17.8 %collective-permute-done.3.half_ref = bf16[768,128]{1,0:T(8,128)(2,1)S(1)} collective-permute-done((bf16[768,128]{1,0:T(8,128)(2,1)S(1)}, bf16[768,128]{1,0:T(8,128)(2,1)S(1)}, u32[]{:S(2)}, u32[]{:S(2)}) %collective-permute-start.3) | collective-permute-done | bytes 196640 | tf_op jit(solution)/shard_map/ppermute | solution.py:158
  57.9 0.0 copy-start.5
  57.9 0.0 collective-permute-done.2
  58.0 0.0 copy-start.2
  58.0 0.0 collective-permute-done.1
  58.0 0.0 copy-start.3
  58.0 0.7 copy-done.5
  58.6 0.2 copy-done.2
  58.8 0.1 copy-done.3
  58.9 2.5 %moment.1 = bf16[4,128,256]{2,1,0:T(8,128)(2,1)} custom-call(s32[1]{0:T(128)} %bitcast.4.z_ref, bf16[1536,128]{1,0:T(8,128)(2,1)} %price.1.own_ref, bf16[1,1536,128]{2,1,0:T(8,128)(2,1)} %bitcast.11, bf16[1,1536,128]{2,1,0:T(8,128)(2,1)} %bitcast.10, bf16[768,128]{1,0:T(8,128)(2,1)} %copy-done.5), custom_call_target="tpu_custom_call" | custom-call | tf_op jit(solution)/shard_map/moment/pallas_call | solution.py:159
  61.4 8.3 %all_to_all.11 = bf16[4,128,256]{2,1,0:T(8,128)(2,1)S(1)} all-to-all(bf16[4,128,256]{2,1,0:T(8,128)(2,1)} %moment.1), channel_id=1, replica_groups=mesh['paths'=4,'cpty'=8] {'paths'}, dimensions={0} | all-to-all | bytes 524288 | tf_op jit(solution)/shard_map/all_to_all | solution.py:168
  69.7 0.0 copy-start
  69.8 2.5 %collective-permute-start.5 = (bf16[128,256]{1,0:T(8,128)(2,1)S(1)}, bf16[128,256]{1,0:T(8,128)(2,1)S(1)}, u32[]{:S(2)}, u32[]{:S(2)}) collective-permute-start(bf16[128,256]{1,0:T(8,128)(2,1)S(1)} %convert_element_type.7), channel_id=1, source_target_pairs={{2,8},{3,9},{4,16},{5,17},{6,24},{7,25},{8,2},{9,3},{12,18},{13,19... | collective-permute-start | bytes 196616 | tf_op jit(solution)/shard_map/ppermute | solution.py:175
  72.3 0.0 copy-done
  72.3 0.8 collective-permute-start.4
  73.1 3.2 %collective-permute-done.4 = bf16[128,128]{1,0:T(8,128)(2,1)S(1)} collective-permute-done((bf16[128,128]{1,0:T(8,128)(2,1)S(1)}, bf16[128,128]{1,0:T(8,128)(2,1)S(1)}, u32[]{:S(2)}, u32[]{:S(2)}) %collective-permute-start.4) | collective-permute-done | bytes 32800 | tf_op jit(solution)/shard_map/ppermute | solution.py:187
  76.3 0.0 copy-start.8
  76.3 2.1 %collective-permute-done.5.crossed_ref = bf16[128,256]{1,0:T(8,128)(2,1)S(1)} collective-permute-done((bf16[128,256]{1,0:T(8,128)(2,1)S(1)}, bf16[128,256]{1,0:T(8,128)(2,1)S(1)}, u32[]{:S(2)}, u32[]{:S(2)}) %collective-permute-start.5) | collective-permute-done | bytes 65568 | tf_op jit(solution)/shard_map/ppermute | solution.py:175
  78.4 0.0 copy-start.7
  78.4 0.0 copy-done.8
  78.4 0.6 copy-done.7
  79.0 1.7 %final.1 = f32[2,128,128]{2,1,0:T(8,128)} custom-call(s32[1]{0:T(128)} %bitcast.3.y_ref, f32[128,256]{1,0:T(8,128)} %copy-done, bf16[1,128,128]{2,1,0:T(8,128)(2,1)} %bitcast.13, bf16[128,256]{1,0:T(8,128)(2,1)} %copy-done.7), custom_call_target="tpu_custom_call" | custom-call | tf_op jit(solution)/shard_map/final/pallas_call | solution.py:194
  (6 shorter events, 0.1 us)
Async XLA Ops:
  0.6 0.7 copy-start.9
  1.3 0.7 copy-start.10
  2.0 0.7 copy-start.11
  8.6 16.3 %copy-start.6 = (bf16[64,1536]{1,0:T(8,128)(2,1)S(1)}, bf16[64,1536]{1,0:T(8,128)(2,1)}, u32[]{:S(2)}) copy-start(bf16[64,1536]{1,0:T(8,128)(2,1)} %param.6) | copy-start | bytes 589828
  24.9 0.9 %copy-start.1 = (bf16[8,72,256]{2,1,0:T(8,128)(2,1)}, bf16[8,72,256]{2,1,0:T(8,128)(2,1)S(1)}, u32[]{:S(2)}) copy-start(bf16[8,72,256]{2,1,0:T(8,128)(2,1)S(1)} %all_to_all.10.mine_ref) | copy-start | bytes 884740
  24.9 1.6 %collective-permute-start = (bf16[8,72,256]{2,1,0:T(8,128)(2,1)S(1)}, bf16[8,72,256]{2,1,0:T(8,128)(2,1)S(1)}, u32[]{:S(2)}, u32[]{:S(2)}) collective-permute-start(bf16[8,72,256]{2,1,0:T(8,128)(2,1)S(1)} %all_to_all.10.mine_ref), channel_id=1, source_target_pairs={{0,8},{8,0},{16,24},{24,16},{1,9},{9,1},{17,25},{25,17},{2,10},{10... | collective-permute-start | bytes 884744 | tf_op jit(solution)/shard_map/ppermute | solution.py:132
  26.4 0.7 copy-start.4
  36.4 21.6 %collective-permute-start.2 = (bf16[1536,128]{1,0:T(8,128)(2,1)}, bf16[1536,128]{1,0:T(8,128)(2,1)S(1)}, u32[]{:S(2)}, u32[]{:S(2)}) collective-permute-start(bf16[1536,128]{1,0:T(8,128)(2,1)} %price.1.own_ref), channel_id=1, source_target_pairs={{0,2},{1,3},{2,4},{3,5},{4,6},{5,7},{6,0},{7,1},{8,10},{9,11},{10,... | collective-permute-start | bytes 1179656 | tf_op jit(solution)/shard_map/ppermute | solution.py:153
  37.0 21.0 %collective-permute-start.1 = (bf16[1536,128]{1,0:T(8,128)(2,1)}, bf16[1536,128]{1,0:T(8,128)(2,1)S(1)}, u32[]{:S(2)}, u32[]{:S(2)}) collective-permute-start(bf16[1536,128]{1,0:T(8,128)(2,1)} %price.1.own_ref), channel_id=1, source_target_pairs={{0,1},{1,0},{2,3},{3,2},{4,5},{5,4},{6,7},{7,6},{8,9},{9,8},{10,11... | collective-permute-start | bytes 1179656 | tf_op jit(solution)/shard_map/ppermute | solution.py:149
  38.5 19.4 %collective-permute-start.3 = (bf16[768,128]{1,0:T(8,128)(2,1)S(1)}, bf16[768,128]{1,0:T(8,128)(2,1)S(1)}, u32[]{:S(2)}, u32[]{:S(2)}) collective-permute-start(bf16[768,128]{1,0:T(8,128)(2,1)S(1)} %constant_dynamic-slice_fusion), channel_id=1, source_target_pairs={{0,4},{1,5},{2,6},{3,7},{4,0},{5,1},{6,2},{7,3},{8,12},{9,13},{10,... | collective-permute-start | bytes 589832 | tf_op jit(solution)/shard_map/ppermute | solution.py:158
  57.9 0.7 copy-start.5
  58.0 0.9 %copy-start.2 = (bf16[1536,128]{1,0:T(8,128)(2,1)}, bf16[1536,128]{1,0:T(8,128)(2,1)S(1)}, u32[]{:S(2)}) copy-start(bf16[1536,128]{1,0:T(8,128)(2,1)S(1)} %collective-permute-done.2) | copy-start | bytes 1179652
  58.0 1.0 %copy-start.3 = (bf16[1536,128]{1,0:T(8,128)(2,1)}, bf16[1536,128]{1,0:T(8,128)(2,1)S(1)}, u32[]{:S(2)}) copy-start(bf16[1536,128]{1,0:T(8,128)(2,1)S(1)} %collective-permute-done.1) | copy-start | bytes 1179652
  69.7 2.6 %copy-start = (f32[128,256]{1,0:T(8,128)}, f32[128,256]{1,0:T(8,128)S(1)}, u32[]{:S(2)}) copy-start(f32[128,256]{1,0:T(8,128)S(1)} %convert_reduce_fusion.own_ref) | copy-start | bytes 393220
  69.8 8.7 %collective-permute-start.5 = (bf16[128,256]{1,0:T(8,128)(2,1)S(1)}, bf16[128,256]{1,0:T(8,128)(2,1)S(1)}, u32[]{:S(2)}, u32[]{:S(2)}) collective-permute-start(bf16[128,256]{1,0:T(8,128)(2,1)S(1)} %convert_element_type.7), channel_id=1, source_target_pairs={{2,8},{3,9},{4,16},{5,17},{6,24},{7,25},{8,2},{9,3},{12,18},{13,19... | collective-permute-start | bytes 196616 | tf_op jit(solution)/shard_map/ppermute | solution.py:175
  72.3 4.0 %collective-permute-start.4 = (bf16[128,128]{1,0:T(8,128)(2,1)S(1)}, bf16[128,128]{1,0:T(8,128)(2,1)S(1)}, u32[]{:S(2)}, u32[]{:S(2)}) collective-permute-start(bf16[128,128]{1,0:T(8,128)(2,1)S(1)} %slice.4), channel_id=1, source_target_pairs={{0,1},{1,0},{2,3},{3,2},{4,5},{5,4},{6,7},{7,6},{8,9},{9,8},{10,11... | collective-permute-start | bytes 98312 | tf_op jit(solution)/shard_map/ppermute | solution.py:187
  76.3 2.1 %copy-start.8 = (bf16[128,128]{1,0:T(8,128)(2,1)}, bf16[128,128]{1,0:T(8,128)(2,1)S(1)}, u32[]{:S(2)}) copy-start(bf16[128,128]{1,0:T(8,128)(2,1)S(1)} %collective-permute-done.4) | copy-start | bytes 98308
  78.4 0.6 copy-start.7

commit v2 on v1

v2 whole, which is shorter than its diff:
```python
import functools

import jax
import jax.numpy as jnp
from jax import lax
from jax.experimental import pallas as pl
from jax.experimental.pallas import tpu as pltpu
from jax.sharding import PartitionSpec as P

CP_DEV = 128
LANES = 128
SUBLANES = 8
CORES = 2
CHUNKS = 2

VMEM = pl.BlockSpec(memory_space=pltpu.VMEM)
SMEM = pl.BlockSpec(memory_space=pltpu.SMEM)
HBM = pl.BlockSpec(memory_space=pltpu.HBM)
BIG = pltpu.CompilerParams(vmem_limit_bytes=48 * 1024 * 1024)


def dot_nt(left, right):
    return lax.dot_general(left, right, (((1,), (1,)), ((), ())), preferred_element_type=jnp.float32)


def dot_tn(left, right):
    return lax.dot_general(left, right, (((0,), (0,)), ((), ())), preferred_element_type=jnp.float32)


def near(array):
    return pltpu.with_memory_space_constraint(array, pltpu.VMEM)


def as_row(blocks):
    return jnp.concatenate([blocks[b:b + 1] for b in range(blocks.shape[0])], axis=1)


def pack_kernel(core_ref, ids_hbm, loadings_hbm, notional_hbm, strike_hbm, curvature_hbm, out_ref, described_ref, ids_ref, terms_ref, sems):
    groups, rows, half = out_ref.shape
    factor_count, trades = loadings_hbm.shape
    copies = [pltpu.make_async_copy(ids_hbm, ids_ref, sems.at[0])]
    for i, source in enumerate((notional_hbm, strike_hbm, curvature_hbm)):
        copies.append(pltpu.make_async_copy(source, terms_ref.at[i], sems.at[1 + i]))
    copies.append(pltpu.make_async_copy(loadings_hbm, described_ref.at[0:factor_count], sems.at[4]))
    for copy in copies:
        copy.start()
    copies[0].wait()
    ids = as_row(ids_ref[...])
    owners = ids // CP_DEV
    marked = lax.broadcasted_iota(jnp.int32, (groups, trades), 0) == owners
    ones = jnp.where(marked, 1.0, 0.0).astype(jnp.bfloat16)
    blocks = trades // LANES
    stacked = jnp.concatenate([ones[:, b * LANES:(b + 1) * LANES] for b in range(blocks)], axis=0)
    upper = lax.broadcasted_iota(jnp.int32, (LANES, LANES), 0) <= lax.broadcasted_iota(jnp.int32, (LANES, LANES), 1)
    counts = jnp.dot(stacked, jnp.where(upper, 1.0, 0.0).astype(jnp.bfloat16), preferred_element_type=jnp.float32)
    before = jnp.zeros((groups, 1), jnp.float32)
    ranks = []
    for b in range(blocks):
        counted = counts[b * groups:(b + 1) * groups] + before
        chosen = jnp.where(marked[:, b * LANES:(b + 1) * LANES], counted, 0.0)
        ranks.append(jnp.sum(chosen, axis=0, keepdims=True))
        before = counted[:, LANES - 1:]
    ranking = jnp.concatenate(ranks, axis=1).astype(jnp.int32) - 1 - core_ref[0] * half
    here = (ranking >= 0) & (ranking < half)
    local_ids = (ids - owners * CP_DEV).astype(jnp.float32)
    for copy in copies[1:4]:
        copy.wait()
    terms = [as_row(terms_ref[i].astype(jnp.float32)) for i in range(3)]
    tail = jnp.concatenate(terms + [local_ids, jnp.zeros((SUBLANES - 4, trades), jnp.float32)], axis=0)
    described_ref[factor_count:rows, :] = tail.astype(jnp.bfloat16)
    copies[4].wait()
    described = described_ref[...]
    slots = lax.broadcasted_iota(jnp.int32, (half, LANES), 0).astype(jnp.float32).astype(jnp.bfloat16)
    for g in range(groups):
        target = jnp.where(here & (owners == g), ranking, -1).astype(jnp.float32).astype(jnp.bfloat16)
        select = jnp.concatenate(
            [
                jnp.where(slots == target[:, b * LANES:(b + 1) * LANES], jnp.bfloat16(1), jnp.bfloat16(0))
                for b in range(blocks)
            ],
            axis=1,
        )
        out_ref[g] = dot_nt(described, select).astype(jnp.bfloat16)


def price_kernel(z_ref, drivers_ref, mine_ref, other_ref, own_ref, far_ref, *, chunk, lines):
    paths = own_ref.shape[0]
    factor_count = drivers_ref.shape[1]
    groups, _, half = mine_ref.shape
    drivers = drivers_ref[chunk * paths:(chunk + 1) * paths]
    total = jnp.zeros((paths, CP_DEV), jnp.float32)
    for ref in (mine_ref, other_ref):
        for g in range(groups):
            slab = ref[g]
            terms = slab[factor_count:].astype(jnp.float32)
            linear = jnp.dot(drivers, slab[:factor_count], preferred_element_type=jnp.float32)
            value = terms[0:1] * (linear + terms[2:3] * jnp.tanh(linear - terms[1:2]))
            ids = terms[3:4].astype(jnp.int32)
            onehot = jnp.where(lax.broadcasted_iota(jnp.int32, (CP_DEV, half), 0) == ids, 1.0, 0.0)
            total = total + dot_nt(value.astype(jnp.bfloat16), onehot.astype(jnp.bfloat16))
    own_ref[...] = jnp.maximum(total, 0.0).astype(jnp.bfloat16)
    start = jnp.where(z_ref[0] < lines // 2, 0, paths // 2)
    far_ref[...] = own_ref[pl.ds(pl.multiple_of(start, LANES), paths // 2), :]


def products(z, own_ref, peer_refs, whole_refs, facing_ref, columns_ref, lines):
    paths, block = own_ref.shape
    columns_ref[:, 0:block] = own_ref[...]
    for e, ref in enumerate(peer_refs):
        columns_ref[:, (e + 1) * block:(e + 2) * block] = ref[...]
    columns = columns_ref[...]
    found = [dot_tn(own_ref[...], columns)]
    found += [dot_tn(ref[...], columns) for ref in whole_refs]
    start = jnp.where(z >= lines // 2, 0, paths // 2)
    facing = columns_ref[pl.ds(pl.multiple_of(start, LANES), paths // 2), :]
    return found + [dot_tn(facing_ref[...], facing)]


def first_kernel(place_ref, own_ref, *refs, lines, depth):
    peer_refs, whole_refs = refs[:depth - 1], refs[depth - 1:depth - 1 + lines // 2 - 1]
    facing_ref, out_ref, columns_ref = refs[-3:]
    for d, product in enumerate(products(place_ref[0], own_ref, peer_refs, whole_refs, facing_ref, columns_ref, lines)):
        out_ref[d] = product


def second_kernel(place_ref, before_ref, own_ref, *refs, lines, depth):
    peer_refs, whole_refs = refs[:depth - 1], refs[depth - 1:depth - 1 + lines // 2 - 1]
    facing_ref, kept_ref, sent_ref, columns_ref, all_ref = refs[-5:]
    z, core = place_ref[0], place_ref[1]
    all_ref[...] = jnp.zeros(all_ref.shape, jnp.float32)
    for d, product in enumerate(products(z, own_ref, peer_refs, whole_refs, facing_ref, columns_ref, lines)):
        all_ref[(z - d + lines) % lines] = before_ref[d] + product
    for i in range(lines // CORES):
        kept_ref[i] = all_ref[i * CORES + core]
        sent_ref[i] = all_ref[i * CORES + (1 - core)].astype(jnp.bfloat16)


def cores_kernel(x_ref, kept_ref, came_ref, own_ref, *sent_refs):
    x, count = x_ref[0], kept_ref.shape[0]
    own_ref[...] = kept_ref[x] + came_ref[x].astype(jnp.float32)
    for e, ref in enumerate(sent_refs):
        i = (x + 1 + e) % count
        ref[...] = (kept_ref[i] + came_ref[i].astype(jnp.float32)).astype(jnp.bfloat16)


def chips_kernel(own_ref, *refs, count):
    total = own_ref[...]
    for ref in refs[:count]:
        total = total + ref[...].astype(jnp.float32)
    refs[count][...] = total
    leaving = total.astype(jnp.bfloat16)
    refs[count + 1][...] = leaving
    block = own_ref.shape[0]
    for e, ref in enumerate(refs[count + 2:]):
        ref[...] = leaving[:, (e + 1) * block:(e + 2) * block]


def final_kernel(y_ref, own_ref, crossed_ref, *refs, scale):
    swapped_refs, out_ref = refs[:-1], refs[-1]
    depth, block, _ = out_ref.shape
    y = y_ref[0]
    for e in range(depth):
        kept = own_ref[:, 0:block] if e == 0 else swapped_refs[e - 1][...].astype(jnp.float32)
        k = (-e) % depth
        turned = crossed_ref[:, k * block:(k + 1) * block].astype(jnp.float32).T
        out_ref[(y + e) % depth] = (kept + turned) * scale


def on_device(factors, loadings, notional, strike, curvature, trade_cpty):
    lines = lax.axis_size("paths")
    groups = lax.axis_size("cpty")
    depth = groups // lines
    chips = lines // CORES
    far = lines // 2
    path_index = lax.axis_index("paths").astype(jnp.int32)
    own_index = lax.axis_index("cpty").astype(jnp.int32)
    x, core = path_index // CORES, path_index % CORES
    z, y = own_index // depth, own_index % depth
    factor_count, trades = loadings.shape
    paths = factors.shape[1]
    half = trades // groups
    rows = factor_count + SUBLANES
    blocks = trades // LANES
    width = depth * CP_DEV
    place = jnp.stack([z, core])

    packed = pl.pallas_call(
        pack_kernel,
        out_shape=pltpu.VMEM((groups, rows, half), jnp.bfloat16),
        in_specs=[SMEM] + [HBM] * 5,
        out_specs=VMEM,
        scratch_shapes=[
            pltpu.VMEM((rows, trades), jnp.bfloat16),
            pltpu.VMEM((blocks, LANES), jnp.int32),
            pltpu.VMEM((3, blocks, LANES), jnp.bfloat16),
            pltpu.SemaphoreType.DMA((5,)),
        ],
        compiler_params=BIG,
        name="pack",
    )(
        core[None],
        trade_cpty.reshape(blocks, LANES),
        loadings,
        notional.reshape(blocks, LANES),
        strike.reshape(blocks, LANES),
        curvature.reshape(blocks, LANES),
    )
    mine = lax.all_to_all(packed, "cpty", split_axis=0, concat_axis=0, tiled=True)
    other = lax.ppermute(mine, "paths", [(i, i ^ 1) for i in range(lines)])

    drivers = near(jnp.transpose(factors))
    everyone = range(groups)
    part = paths // CHUNKS
    owns, met = [], []
    for chunk in range(CHUNKS):
        own, leaving = pl.pallas_call(
            functools.partial(price_kernel, chunk=chunk, lines=lines),
            out_shape=(
                pltpu.VMEM((part, CP_DEV), jnp.bfloat16),
                pltpu.VMEM((part // 2, CP_DEV), jnp.bfloat16),
            ),
            in_specs=[SMEM, VMEM, VMEM, VMEM],
            out_specs=(VMEM, VMEM),
            compiler_params=BIG,
            name=f"price{chunk}",
        )(z[None], drivers, near(mine), near(other))
        peers = [
            lax.ppermute(own, "cpty", [(c, c - c % depth + (c + e) % depth) for c in everyone])
            for e in range(1, depth)
        ]
        wholes = [
            lax.ppermute(own, "cpty", [(c, (c + d * depth) % groups) for c in everyone])
            for d in range(1, far)
        ]
        facing = lax.ppermute(leaving, "cpty", [(c, (c + far * depth) % groups) for c in everyone])
        owns.append(own)
        met.append([near(a) for a in [own, *peers, *wholes, facing]])

    count = len(met[0])
    columns = pltpu.VMEM((part, width), jnp.bfloat16)
    before = pl.pallas_call(
        functools.partial(first_kernel, lines=lines, depth=depth),
        out_shape=pltpu.VMEM((far + 1, CP_DEV, width), jnp.float32),
        in_specs=[SMEM] + [VMEM] * count,
        out_specs=VMEM,
        scratch_shapes=[columns],
        compiler_params=BIG,
        name="moment0",
    )(place, *met[0])
    kept, sent = pl.pallas_call(
        functools.partial(second_kernel, lines=lines, depth=depth),
        out_shape=(
            pltpu.VMEM((chips, CP_DEV, width), jnp.float32),
            pltpu.VMEM((chips, CP_DEV, width), jnp.bfloat16),
        ),
        in_specs=[SMEM] + [VMEM] * (count + 1),
        out_specs=(VMEM, VMEM),
        scratch_shapes=[columns, pltpu.VMEM((lines, CP_DEV, width), jnp.float32)],
        compiler_params=BIG,
        name="moment1",
    )(place, near(before), *met[1])
    came = lax.ppermute(sent, "paths", [(i, i ^ 1) for i in range(lines)])
    out = pl.pallas_call(
        cores_kernel,
        out_shape=[pltpu.VMEM((CP_DEV, width), jnp.float32)]
        + [pltpu.VMEM((CP_DEV, width), jnp.bfloat16)] * (chips - 1),
        in_specs=[SMEM, VMEM, VMEM],
        out_specs=[VMEM] * chips,
        compiler_params=BIG,
        name="cores",
    )(x[None], near(kept), near(came))
    arrived = [
        lax.ppermute(out[e], "paths", [(i, (i + e * CORES) % lines) for i in range(lines)])
        for e in range(1, chips)
    ]
    total, leaving, *swaps = pl.pallas_call(
        functools.partial(chips_kernel, count=chips - 1),
        out_shape=[
            pltpu.VMEM((CP_DEV, width), jnp.float32),
            pltpu.VMEM((CP_DEV, width), jnp.bfloat16),
        ]
        + [pltpu.VMEM((CP_DEV, CP_DEV), jnp.bfloat16)] * (depth - 1),
        in_specs=[VMEM] * chips,
        out_specs=[VMEM] * (depth + 1),
        compiler_params=BIG,
        name="chips",
    )(near(out[0]), *[near(a) for a in arrived])

    def flat(p, zz, yy):
        return p * groups + zz * depth + yy

    crossed = lax.ppermute(
        leaving,
        ("paths", "cpty"),
        [
            (flat(a, b, yy), flat(b, a, yy))
            for a in range(lines)
            for b in range(lines)
            for yy in range(depth)
            if a != b
        ],
    )
    swapped = [
        lax.ppermute(swaps[e - 1], "cpty", [(c, c - c % depth + (c - e) % depth) for c in everyone])
        for e in range(1, depth)
    ]
    moment = pl.pallas_call(
        functools.partial(final_kernel, scale=1.0 / (paths * lines)),
        out_shape=jax.ShapeDtypeStruct((depth, CP_DEV, CP_DEV), jnp.float32),
        in_specs=[SMEM] + [VMEM] * (depth + 1),
        out_specs=VMEM,
        compiler_params=BIG,
        name="final",
    )(y[None], near(total), near(crossed), *[near(a) for a in swapped])
    return jnp.concatenate(owns, axis=0), moment.reshape(depth * CP_DEV, CP_DEV)


def solution(mesh):
    in_specs = (P(None, "paths"), P(None, "cpty"), P("cpty"), P("cpty"), P("cpty"), P("cpty"))
    out_specs = (P("paths", "cpty"), P("paths", "cpty"))
    return jax.shard_map(on_device, mesh=mesh, in_specs=in_specs, out_specs=out_specs, check_vma=False)
```

time: 81.2 us -> 68 us (0.84)
  blocking collectives: 24.6 us -> 16.1 us
  Pallas kernels: 18.6 us -> 13.7 us
  local copies, waits for them, and re-layouts: 6.25 us -> 1.87 us
  starting transfers between devices: 6.07 us -> 9.25 us
  waiting for transfers between devices: 23.8 us -> 25.2 us
    all_to_all x1 -> x0, blocking collectives: 8.27 us -> none  [on_device(): lax.all_to_all(partial, 'paths', split_axis=0, concat_axis=0, tiled=True)]
    pallas_call x3 -> x7, Pallas kernels: 16.9 us -> 12.9 us  [the longest x2 7.12 us: on_device(): pl.pallas_call(functools.partial(price_kernel, chunk=chunk, lines=lines),...]
    ppermute x4 -> x9, starting transfers between devices: 3.54 us -> 7.1 us  [the longest x2 2.85 us: on_device(): lax.ppermute(own, 'cpty', [(c, (c + d * depth) % groups) for c in everyone])]
    unnamed x25 -> x13, local copies, waits for them, and re-layouts: 5.26 us -> 1.87 us
    ppermute x1, waiting for transfers between devices: 2.12 us -> 4.75 us  [on_device(): lax.ppermute(leaving, ('paths', 'cpty'), [(flat(a, b, yy), flat(b, a, yy)...]
    ppermute x4 -> x9, waiting for transfers between devices: 21.1 us -> 19.1 us  [the longest x2 13.8 us: on_device(): lax.ppermute(leaving, 'cpty', [(c, (c + far * depth) % groups) for c in e...]
    dynamic_slice x1 -> x0, local copies, waits for them, and re-layouts: 0.97 us -> none  [on_device(): lax.dynamic_slice_in_dim(exposure, jnp.where(z < far, 0, paths // 2), pat...]
    pallas_call x1, Pallas kernels: 1.68 us -> 0.76 us  [on_device(): pl.pallas_call(functools.partial(final_kernel, scale=1.0 / (paths * lines...]
  transfers between devices with their start and end apart: 6 -> 11, of which waited for: 4 -> 7; matrix products, arithmetic and copies ran while one was open for 2% -> 2% of each run, Pallas kernels for 0% -> 7%
where the time goes in v2:
time: 68 us; the launch traced here: 67.7 us
  waiting for transfers between devices  25.2 us (37%)
  blocking collectives  16.1 us (24%)
  Pallas kernels  13.7 us (20%)
  starting transfers between devices  9.25 us (14%)
  local copies, waits for them, and re-layouts  1.87 us (3%)
  other arithmetic  0.85 us (1%)
  between operations  0.79 us (1%)
    all_to_all x1, blocking collectives, on_device(): lax.all_to_all(packed, 'cpty', split_axis=0, concat_axis=0, tiled=True)  16.1 us
    ppermute x2, waiting for transfers between devices, on_device(): lax.ppermute(leaving, 'cpty', [(c, (c + far * depth) % groups) for c in e...  13.8 us
    pallas_call x2, Pallas kernels, on_device(): pl.pallas_call(functools.partial(price_kernel, chunk=chunk, lines=lines),...  7.12 us
    ppermute x1, waiting for transfers between devices, on_device(): lax.ppermute(leaving, ('paths', 'cpty'), [(flat(a, b, yy), flat(b, a, yy)...  4.75 us
    pallas_call x1, Pallas kernels, on_device(): pl.pallas_call(pack_kernel, out_shape=pltpu.VMEM((groups, rows, half), jn...  3.92 us
    ppermute x1, waiting for transfers between devices, on_device(): lax.ppermute(out[e], 'paths', [(i, (i + e * CORES) % lines) for i in rang...  3.73 us
    ppermute x2, starting transfers between devices, on_device(): lax.ppermute(own, 'cpty', [(c, (c + d * depth) % groups) for c in everyone])  2.85 us
    ppermute x1, starting transfers between devices, on_device(): lax.ppermute(leaving, ('paths', 'cpty'), [(flat(a, b, yy), flat(b, a, yy)...  2.15 us
  transfers between devices with their start and end apart: 11, of which 7 were waited for; matrix products, arithmetic and copies ran while one was open for 2% of the time, Pallas kernels for 7%

profile of v2, /device:TPU:2, one launch (start us, length us, event | category | flops | bytes accessed | tf_op | source)
XLA Modules:
  0.0 67.7 jit_solution(6600056442121935367)
XLA Ops:
  0.6 0.0 copy-start.4
  0.6 0.0 copy-start.3
  0.7 0.0 copy-start.1
  0.7 0.0 copy-start.2
  0.7 0.6 copy-done.4
  1.3 0.0 copy-done.3
  1.3 0.0 copy-done.1
  1.4 0.0 copy-done.2
  1.4 0.0 copy-start
  1.4 0.9 %copy-done = bf16[64,2048]{1,0:T(8,128)(2,1)S(1)} copy-done((bf16[64,2048]{1,0:T(8,128)(2,1)S(1)}, bf16[64,2048]{1,0:T(8,128)(2,1)}, u32[]{:S(2)}) %copy-start) | copy-done | bytes 262168
  2.3 3.9 %pack.1 = bf16[8,72,256]{2,1,0:T(8,128)(2,1)S(1)} custom-call(s32[1]{0:T(128)} %bitcast.2.core_ref, s32[16,128]{1,0:T(8,128)S(1)} %bitcast.12, bf16[64,2048]{1,0:T(8,128)(2,1)S(1)} %copy-done, bf16[16,128]{1,0:T(8,128)(2,1)S(1)} %bitcast.13, bf16[16,128]{1,0:T(8,128)(2,1)S(1)} %bitcast.14, bf16[16,128]{1,0:T(8,128)(2,1)S(1)} %bitcast.15), custom_call_target="tpu_custom_call" | custom-call | tf_op jit(solution)/shard_map/pack/pallas_call | solution.py:187
  6.3 0.0 copy-start.5
  6.3 16.1 %all_to_all.5.mine_ref = bf16[8,72,256]{2,1,0:T(8,128)(2,1)S(1)} all-to-all(bf16[8,72,256]{2,1,0:T(8,128)(2,1)S(1)} %pack.1), channel_id=1, replica_groups=mesh['paths'=4,'cpty'=8] {'cpty'}, dimensions={0} | all-to-all | bytes 589824 | tf_op jit(solution)/shard_map/all_to_all | solution.py:208
  22.4 0.0 collective-permute-start
  22.4 0.0 copy-done.5
  22.4 0.2 copy.8
  22.6 1.3 %collective-permute-done.other_ref = bf16[8,72,256]{2,1,0:T(8,128)(2,1)S(1)} collective-permute-done((bf16[8,72,256]{2,1,0:T(8,128)(2,1)S(1)}, bf16[8,72,256]{2,1,0:T(8,128)(2,1)S(1)}, u32[]{:S(2)}, u32[]{:S(2)}) %collective-permute-start) | collective-permute-done | bytes 294944 | tf_op jit(solution)/shard_map/ppermute | solution.py:209
  23.9 3.6 %price0.1 = (bf16[768,128]{1,0:T(8,128)(2,1)S(1)}, bf16[384,128]{1,0:T(8,128)(2,1)S(1)}) custom-call(s32[1]{0:T(128)} %bitcast.z_ref, bf16[1536,64]{1,0:T(8,128)(2,1)S(1)} %bitcast.10, bf16[8,72,256]{2,1,0:T(8,128)(2,1)S(1)} %all_to_all.5.mine_ref, bf16[8,72,256]{2,1,0:T(8,128)(2,1)S(1)} %collective-permute-done.other_ref), custom_call_target="tpu_custom_call" | custom-call | tf_op jit(solution)/shard_map/price0/pallas_call | solution.py:216
  27.5 0.8 %collective-permute-start.3 = (bf16[384,128]{1,0:T(8,128)(2,1)S(1)}, bf16[384,128]{1,0:T(8,128)(2,1)S(1)}, u32[]{:S(2)}, u32[]{:S(2)}) collective-permute-start(bf16[384,128]{1,0:T(8,128)(2,1)S(1)} %get-tuple-element.15), channel_id=1, source_target_pairs={{0,4},{1,5},{2,6},{3,7},{4,0},{5,1},{6,2},{7,3},{8,12},{9,13},{10,... | collective-permute-start | bytes 294920 | tf_op jit(solution)/shard_map/ppermute | solution.py:235
  28.3 1.4 %collective-permute-start.2 = (bf16[768,128]{1,0:T(8,128)(2,1)S(1)}, bf16[768,128]{1,0:T(8,128)(2,1)S(1)}, u32[]{:S(2)}, u32[]{:S(2)}) collective-permute-start(bf16[768,128]{1,0:T(8,128)(2,1)S(1)} %get-tuple-element.13.own_ref), channel_id=1, source_target_pairs={{0,2},{1,3},{2,4},{3,5},{4,6},{5,7},{6,0},{7,1},{8,10},{9,11},{10,... | collective-permute-start | bytes 589832 | tf_op jit(solution)/shard_map/ppermute | solution.py:232
  29.6 0.7 %collective-permute-start.1 = (bf16[768,128]{1,0:T(8,128)(2,1)S(1)}, bf16[768,128]{1,0:T(8,128)(2,1)S(1)}, u32[]{:S(2)}, u32[]{:S(2)}) collective-permute-start(bf16[768,128]{1,0:T(8,128)(2,1)S(1)} %get-tuple-element.13.own_ref), channel_id=1, source_target_pairs={{0,1},{1,0},{2,3},{3,2},{4,5},{5,4},{6,7},{7,6},{8,9},{9,8},{10,11... | collective-permute-start | bytes 589832 | tf_op jit(solution)/shard_map/ppermute | solution.py:228
  30.3 3.6 %price1.1 = (bf16[768,128]{1,0:T(8,128)(2,1)S(1)}, bf16[384,128]{1,0:T(8,128)(2,1)S(1)}) custom-call(s32[1]{0:T(128)} %bitcast.z_ref, bf16[1536,64]{1,0:T(8,128)(2,1)S(1)} %bitcast.11, bf16[8,72,256]{2,1,0:T(8,128)(2,1)S(1)} %all_to_all.5.mine_ref, bf16[8,72,256]{2,1,0:T(8,128)(2,1)S(1)} %collective-permute-done.other_ref), custom_call_target="tpu_custom_call" | custom-call | tf_op jit(solution)/shard_map/price1/pallas_call | solution.py:216
  33.9 1.5 %collective-permute-start.5 = (bf16[768,128]{1,0:T(8,128)(2,1)S(1)}, bf16[768,128]{1,0:T(8,128)(2,1)S(1)}, u32[]{:S(2)}, u32[]{:S(2)}) collective-permute-start(bf16[768,128]{1,0:T(8,128)(2,1)S(1)} %get-tuple-element.14.own_ref), channel_id=1, source_target_pairs={{0,2},{1,3},{2,4},{3,5},{4,6},{5,7},{6,0},{7,1},{8,10},{9,11},{10,... | collective-permute-start | bytes 589832 | tf_op jit(solution)/shard_map/ppermute | solution.py:232
  35.4 1.3 %collective-permute-start.4 = (bf16[768,128]{1,0:T(8,128)(2,1)S(1)}, bf16[768,128]{1,0:T(8,128)(2,1)S(1)}, u32[]{:S(2)}, u32[]{:S(2)}) collective-permute-start(bf16[768,128]{1,0:T(8,128)(2,1)S(1)} %get-tuple-element.14.own_ref), channel_id=1, source_target_pairs={{0,1},{1,0},{2,3},{3,2},{4,5},{5,4},{6,7},{7,6},{8,9},{9,8},{10,11... | collective-permute-start | bytes 589832 | tf_op jit(solution)/shard_map/ppermute | solution.py:228
  36.7 9.2 %collective-permute-done.3.refs_2_ = bf16[384,128]{1,0:T(8,128)(2,1)S(1)} collective-permute-done((bf16[384,128]{1,0:T(8,128)(2,1)S(1)}, bf16[384,128]{1,0:T(8,128)(2,1)S(1)}, u32[]{:S(2)}, u32[]{:S(2)}) %collective-permute-start.3) | collective-permute-done | bytes 98336 | tf_op jit(solution)/shard_map/ppermute | solution.py:235
  46.0 0.0 collective-permute-start.6
  46.0 0.1 pad_add_fusion.place_ref
  46.0 0.0 collective-permute-done.2.refs_1_
  46.0 0.0 collective-permute-done.1.refs_0_
  46.0 0.9 %moment0.1.before_ref = f32[3,128,256]{2,1,0:T(8,128)S(1)} custom-call(s32[2]{0:T(128)S(1)} %pad_add_fusion.place_ref, bf16[768,128]{1,0:T(8,128)(2,1)S(1)} %get-tuple-element.13.own_ref, bf16[768,128]{1,0:T(8,128)(2,1)S(1)} %collective-permute-done.1.refs_0_, bf16[768,128]{1,0:T(8,128)(2,1)S(1)} %collective-permute-done.2.refs_1_, ...), custom_call_target="tpu_custom_call" | custom-call | tf_op jit(solution)/shard_map/moment0/pallas_call | solution.py:241
  47.0 4.5 %collective-permute-done.6.refs_2_ = bf16[384,128]{1,0:T(8,128)(2,1)S(1)} collective-permute-done((bf16[384,128]{1,0:T(8,128)(2,1)S(1)}, bf16[384,128]{1,0:T(8,128)(2,1)S(1)}, u32[]{:S(2)}, u32[]{:S(2)}) %collective-permute-start.6) | collective-permute-done | bytes 98336 | tf_op jit(solution)/shard_map/ppermute | solution.py:235
  51.5 0.0 collective-permute-done.5.refs_1_
  51.5 0.0 collective-permute-done.4.refs_0_
  51.5 0.9 %moment1.1 = (f32[2,128,256]{2,1,0:T(8,128)S(1)}, bf16[2,128,256]{2,1,0:T(8,128)(2,1)S(1)}) custom-call(s32[2]{0:T(128)S(1)} %pad_add_fusion.place_ref, f32[3,128,256]{2,1,0:T(8,128)S(1)} %moment0.1.before_ref, bf16[768,128]{1,0:T(8,128)(2,1)S(1)} %get-tuple-element.14.own_ref, bf16[768,128]{1,0:T(8,128)(2,1)S(1)} %collective-permute-done.4.refs_0_, ...), custom_call_target="tpu_custom_call" | custom-call | tf_op jit(solution)/shard_map/moment1/pallas_call | solution.py:250
  52.4 0.1 collective-permute-start.7
  52.5 1.3 %collective-permute-done.7.came_ref = bf16[2,128,256]{2,1,0:T(8,128)(2,1)S(1)} collective-permute-done((bf16[2,128,256]{2,1,0:T(8,128)(2,1)S(1)}, bf16[2,128,256]{2,1,0:T(8,128)(2,1)S(1)}, u32[]{:S(2)}, u32[]{:S(2)}) %collective-permute-start.7) | collective-permute-done | bytes 131104 | tf_op jit(solution)/shard_map/ppermute | solution.py:262
  53.9 0.6 collective-permute-start.8
  54.5 3.7 %collective-permute-done.8.refs_0_ = bf16[128,256]{1,0:T(8,128)(2,1)S(1)} collective-permute-done((bf16[128,256]{1,0:T(8,128)(2,1)S(1)}, bf16[128,256]{1,0:T(8,128)(2,1)S(1)}, u32[]{:S(2)}, u32[]{:S(2)}) %collective-permute-start.8) | collective-permute-done | bytes 65568 | tf_op jit(solution)/shard_map/ppermute | solution.py:273
  58.2 0.8 %collective-permute-start.10 = (bf16[128,128]{1,0:T(8,128)(2,1)S(1)}, bf16[128,128]{1,0:T(8,128)(2,1)S(1)}, u32[]{:S(2)}, u32[]{:S(2)}) collective-permute-start(bf16[128,128]{1,0:T(8,128)(2,1)S(1)} %get-tuple-element.23), channel_id=1, source_target_pairs={{0,1},{1,0},{2,3},{3,2},{4,5},{5,4},{6,7},{7,6},{8,9},{9,8},{10,11... | collective-permute-start | bytes 98312 | tf_op jit(solution)/shard_map/ppermute | solution.py:304
  59.0 2.2 %collective-permute-start.9 = (bf16[128,256]{1,0:T(8,128)(2,1)S(1)}, bf16[128,256]{1,0:T(8,128)(2,1)S(1)}, u32[]{:S(2)}, u32[]{:S(2)}) collective-permute-start(bf16[128,256]{1,0:T(8,128)(2,1)S(1)} %get-tuple-element.22), channel_id=1, source_target_pairs={{2,8},{3,9},{4,16},{5,17},{6,24},{7,25},{8,2},{9,3},{12,18},{13,19... | collective-permute-start | bytes 196616 | tf_op jit(solution)/shard_map/ppermute | solution.py:292
  61.2 0.8 %pad_maximum_fusion = bf16[1536,128]{1,0:T(8,128)(2,1)} fusion(bf16[768,128]{1,0:T(8,128)(2,1)S(1)} %get-tuple-element.14.own_ref, bf16[768,128]{1,0:T(8,128)(2,1)S(1)} %get-tuple-element.13.own_ref), kind=kLoop, calls=%fused_computation | loop fusion | flops 786432 | bytes 786432 | tf_op jit(solution)/shard_map/concatenate | solution.py:315
  61.9 0.3 collective-permute-done.10.refs_0_
  62.2 4.8 %collective-permute-done.9.crossed_ref = bf16[128,256]{1,0:T(8,128)(2,1)S(1)} collective-permute-done((bf16[128,256]{1,0:T(8,128)(2,1)S(1)}, bf16[128,256]{1,0:T(8,128)(2,1)S(1)}, u32[]{:S(2)}, u32[]{:S(2)}) %collective-permute-start.9) | collective-permute-done | bytes 65568 | tf_op jit(solution)/shard_map/ppermute | solution.py:292
  67.0 0.8 %final.1 = f32[2,128,128]{2,1,0:T(8,128)} custom-call(s32[1]{0:T(128)} %bitcast.7.y_ref, f32[128,256]{1,0:T(8,128)S(1)} %get-tuple-element.21.own_ref, bf16[128,256]{1,0:T(8,128)(2,1)S(1)} %collective-permute-done.9.crossed_ref, bf16[128,128]{1,0:T(8,128)(2,1)S(1)} %collective-permute-done.10.refs_0_), custom_call_target="tpu_custom_call" | custom-call | tf_op jit(solution)/shard_map/final/pallas_call | solution.py:307
  (2 shorter events, 0.0 us)
Async XLA Ops:
  0.6 0.7 %copy-start.4 = (bf16[2048]{0:T(1024)(128)(2,1)S(1)}, bf16[2048]{0:T(1024)(128)(2,1)}, u32[]{:S(2)}) copy-start(bf16[2048]{0:T(1024)(128)(2,1)} %param.10) | copy-start | bytes 12292
  0.6 0.7 %copy-start.3 = (bf16[2048]{0:T(1024)(128)(2,1)S(1)}, bf16[2048]{0:T(1024)(128)(2,1)}, u32[]{:S(2)}) copy-start(bf16[2048]{0:T(1024)(128)(2,1)} %param.9) | copy-start | bytes 12292
  0.7 0.7 %copy-start.1 = (s32[2048]{0:T(1024)S(1)}, s32[2048]{0:T(1024)}, u32[]{:S(2)}) copy-start(s32[2048]{0:T(1024)} %param.11) | copy-start | bytes 24580
  0.7 0.7 %copy-start.2 = (bf16[2048]{0:T(1024)(128)(2,1)S(1)}, bf16[2048]{0:T(1024)(128)(2,1)}, u32[]{:S(2)}) copy-start(bf16[2048]{0:T(1024)(128)(2,1)} %param.8) | copy-start | bytes 12292
  1.4 0.9 %copy-start = (bf16[64,2048]{1,0:T(8,128)(2,1)S(1)}, bf16[64,2048]{1,0:T(8,128)(2,1)}, u32[]{:S(2)}) copy-start(bf16[64,2048]{1,0:T(8,128)(2,1)} %loadings_hbm.1) | copy-start | bytes 786436
  6.3 16.1 %copy-start.5 = (bf16[64,1536]{1,0:T(8,128)(2,1)S(1)}, bf16[64,1536]{1,0:T(8,128)(2,1)}, u32[]{:S(2)}) copy-start(bf16[64,1536]{1,0:T(8,128)(2,1)} %param.6) | copy-start | bytes 589828
  22.4 1.6 %collective-permute-start = (bf16[8,72,256]{2,1,0:T(8,128)(2,1)S(1)}, bf16[8,72,256]{2,1,0:T(8,128)(2,1)S(1)}, u32[]{:S(2)}, u32[]{:S(2)}) collective-permute-start(bf16[8,72,256]{2,1,0:T(8,128)(2,1)S(1)} %all_to_all.5.mine_ref), channel_id=1, source_target_pairs={{0,8},{8,0},{16,24},{24,16},{1,9},{9,1},{17,25},{25,17},{2,10},{10... | collective-permute-start | bytes 884744 | tf_op jit(solution)/shard_map/ppermute | solution.py:209
  27.5 18.4 %collective-permute-start.3 = (bf16[384,128]{1,0:T(8,128)(2,1)S(1)}, bf16[384,128]{1,0:T(8,128)(2,1)S(1)}, u32[]{:S(2)}, u32[]{:S(2)}) collective-permute-start(bf16[384,128]{1,0:T(8,128)(2,1)S(1)} %get-tuple-element.15), channel_id=1, source_target_pairs={{0,4},{1,5},{2,6},{3,7},{4,0},{5,1},{6,2},{7,3},{8,12},{9,13},{10,... | collective-permute-start | bytes 294920 | tf_op jit(solution)/shard_map/ppermute | solution.py:235
  28.3 17.8 %collective-permute-start.2 = (bf16[768,128]{1,0:T(8,128)(2,1)S(1)}, bf16[768,128]{1,0:T(8,128)(2,1)S(1)}, u32[]{:S(2)}, u32[]{:S(2)}) collective-permute-start(bf16[768,128]{1,0:T(8,128)(2,1)S(1)} %get-tuple-element.13.own_ref), channel_id=1, source_target_pairs={{0,2},{1,3},{2,4},{3,5},{4,6},{5,7},{6,0},{7,1},{8,10},{9,11},{10,... | collective-permute-start | bytes 589832 | tf_op jit(solution)/shard_map/ppermute | solution.py:232
  29.6 16.4 %collective-permute-start.1 = (bf16[768,128]{1,0:T(8,128)(2,1)S(1)}, bf16[768,128]{1,0:T(8,128)(2,1)S(1)}, u32[]{:S(2)}, u32[]{:S(2)}) collective-permute-start(bf16[768,128]{1,0:T(8,128)(2,1)S(1)} %get-tuple-element.13.own_ref), channel_id=1, source_target_pairs={{0,1},{1,0},{2,3},{3,2},{4,5},{5,4},{6,7},{7,6},{8,9},{9,8},{10,11... | collective-permute-start | bytes 589832 | tf_op jit(solution)/shard_map/ppermute | solution.py:228
  33.9 17.6 %collective-permute-start.5 = (bf16[768,128]{1,0:T(8,128)(2,1)S(1)}, bf16[768,128]{1,0:T(8,128)(2,1)S(1)}, u32[]{:S(2)}, u32[]{:S(2)}) collective-permute-start(bf16[768,128]{1,0:T(8,128)(2,1)S(1)} %get-tuple-element.14.own_ref), channel_id=1, source_target_pairs={{0,2},{1,3},{2,4},{3,5},{4,6},{5,7},{6,0},{7,1},{8,10},{9,11},{10,... | collective-permute-start | bytes 589832 | tf_op jit(solution)/shard_map/ppermute | solution.py:232
  35.4 16.1 %collective-permute-start.4 = (bf16[768,128]{1,0:T(8,128)(2,1)S(1)}, bf16[768,128]{1,0:T(8,128)(2,1)S(1)}, u32[]{:S(2)}, u32[]{:S(2)}) collective-permute-start(bf16[768,128]{1,0:T(8,128)(2,1)S(1)} %get-tuple-element.14.own_ref), channel_id=1, source_target_pairs={{0,1},{1,0},{2,3},{3,2},{4,5},{5,4},{6,7},{7,6},{8,9},{9,8},{10,11... | collective-permute-start | bytes 589832 | tf_op jit(solution)/shard_map/ppermute | solution.py:228
  46.0 5.5 %collective-permute-start.6 = (bf16[384,128]{1,0:T(8,128)(2,1)S(1)}, bf16[384,128]{1,0:T(8,128)(2,1)S(1)}, u32[]{:S(2)}, u32[]{:S(2)}) collective-permute-start(bf16[384,128]{1,0:T(8,128)(2,1)S(1)} %get-tuple-element.16), channel_id=1, source_target_pairs={{0,4},{1,5},{2,6},{3,7},{4,0},{5,1},{6,2},{7,3},{8,12},{9,13},{10,... | collective-permute-start | bytes 294920 | tf_op jit(solution)/shard_map/ppermute | solution.py:235
  52.4 1.4 %collective-permute-start.7 = (bf16[2,128,256]{2,1,0:T(8,128)(2,1)S(1)}, bf16[2,128,256]{2,1,0:T(8,128)(2,1)S(1)}, u32[]{:S(2)}, u32[]{:S(2)}) collective-permute-start(bf16[2,128,256]{2,1,0:T(8,128)(2,1)S(1)} %get-tuple-element.18), channel_id=1, source_target_pairs={{0,8},{8,0},{16,24},{24,16},{1,9},{9,1},{17,25},{25,17},{2,10},{10... | collective-permute-start | bytes 393224 | tf_op jit(solution)/shard_map/ppermute | solution.py:262
  53.9 4.3 %collective-permute-start.8 = (bf16[128,256]{1,0:T(8,128)(2,1)S(1)}, bf16[128,256]{1,0:T(8,128)(2,1)S(1)}, u32[]{:S(2)}, u32[]{:S(2)}) collective-permute-start(bf16[128,256]{1,0:T(8,128)(2,1)S(1)} %get-tuple-element.20), channel_id=1, source_target_pairs={{0,16},{8,24},{16,0},{24,8},{1,17},{9,25},{17,1},{25,9},{2,18},{10... | collective-permute-start | bytes 196616 | tf_op jit(solution)/shard_map/ppermute | solution.py:273
  58.2 4.0 %collective-permute-start.10 = (bf16[128,128]{1,0:T(8,128)(2,1)S(1)}, bf16[128,128]{1,0:T(8,128)(2,1)S(1)}, u32[]{:S(2)}, u32[]{:S(2)}) collective-permute-start(bf16[128,128]{1,0:T(8,128)(2,1)S(1)} %get-tuple-element.23), channel_id=1, source_target_pairs={{0,1},{1,0},{2,3},{3,2},{4,5},{5,4},{6,7},{7,6},{8,9},{9,8},{10,11... | collective-permute-start | bytes 98312 | tf_op jit(solution)/shard_map/ppermute | solution.py:304
  59.0 7.9 %collective-permute-start.9 = (bf16[128,256]{1,0:T(8,128)(2,1)S(1)}, bf16[128,256]{1,0:T(8,128)(2,1)S(1)}, u32[]{:S(2)}, u32[]{:S(2)}) collective-permute-start(bf16[128,256]{1,0:T(8,128)(2,1)S(1)} %get-tuple-element.22), channel_id=1, source_target_pairs={{2,8},{3,9},{4,16},{5,17},{6,24},{7,25},{8,2},{9,3},{12,18},{13,19... | collective-permute-start | bytes 196616 | tf_op jit(solution)/shard_map/ppermute | solution.py:292
